TPU v7x, 32 devices: a whole 2x2x4 slice. The times are simulated.
32 devices in a mesh: ep: 32 (over z, y, x, core).
Axes of the slice: x: 2, y: 2, z: 4, core: 2. Of those that a mesh axis runs over, the one named last changes fastest.
Arguments:
- hidden: bfloat16 [65536, 1024], P('ep')
- w_router: float32 [1024, 32], replicated
- expert_ids: int32 [65536, 2], P('ep')
- w_one: bfloat16 [32, 1024, 2816], P('ep')
- w_three: bfloat16 [32, 1024, 2816], P('ep')
- w_two: bfloat16 [32, 2816, 1024], P('ep')
Outputs:
- output: bfloat16 [65536, 1024], P('ep')
All inputs are finite; a program needn't handle non-finite values.
Results may differ from a plain program's by a relative error of at most 0.00868986.
Values are sent between devices in bfloat16 or wider.
A program may use at most 1 GiB of HBM per device.

v0:
```python
import jax
import jax.numpy as jnp
from jax import lax
from jax.sharding import PartitionSpec as P


def route_gates(hidden_loc, w_router, ids_loc):
    logits = jnp.dot(hidden_loc.astype(jnp.float32), w_router, preferred_element_type=jnp.float32)
    prob_vals = jax.nn.softmax(logits, axis=-1)
    picked = jnp.take_along_axis(prob_vals, ids_loc, axis=1)
    return picked / jnp.sum(picked, axis=1, keepdims=True)


def expert_ffn(sorted_rows, group_sizes, w_one, w_three, w_two):
    h_one = lax.ragged_dot(sorted_rows, w_one, group_sizes, preferred_element_type=jnp.float32)
    h_three = lax.ragged_dot(sorted_rows, w_three, group_sizes, preferred_element_type=jnp.float32)
    act_rows = (jax.nn.silu(h_one) * h_three).astype(jnp.bfloat16)
    return lax.ragged_dot(act_rows, w_two, group_sizes, preferred_element_type=jnp.float32).astype(jnp.bfloat16)


def solution(mesh):
    dev_count = mesh.shape["ep"]

    def device_body(hidden_loc, w_router, ids_loc, w_one, w_three, w_two):
        tok_count = hidden_loc.shape[0]
        model_dim = hidden_loc.shape[1]
        local_count = w_one.shape[0]
        row_cap = 4 * tok_count // dev_count
        gate_vals = route_gates(hidden_loc, w_router, ids_loc)
        flat_ids = ids_loc.reshape(-1)
        assign_count = flat_ids.shape[0]
        dest_dev = flat_ids // local_count
        dest_onehot = (dest_dev[:, None] == jnp.arange(dev_count)[None, :]).astype(jnp.int32)
        slot_idx = jnp.sum(jnp.cumsum(dest_onehot, axis=0) * dest_onehot, axis=1) - 1
        slot_pos = dest_dev * row_cap + slot_idx
        src_token = jnp.zeros((dev_count * row_cap,), jnp.int32).at[slot_pos].set(jnp.arange(assign_count, dtype=jnp.int32) // 2)
        send_exp = jnp.full((dev_count * row_cap,), local_count, jnp.int32).at[slot_pos].set(flat_ids % local_count)
        send_rows = jnp.take(hidden_loc, src_token, axis=0).reshape(dev_count, row_cap, model_dim)
        recv_rows = lax.all_to_all(send_rows, "ep", 0, 0, tiled=True)
        recv_exp = lax.all_to_all(send_exp.reshape(dev_count, row_cap), "ep", 0, 0, tiled=True)
        row_exp = recv_exp.reshape(-1)
        sort_order = jnp.argsort(row_exp, stable=True)
        group_sizes = jnp.sum((row_exp[:, None] == jnp.arange(local_count)[None, :]).astype(jnp.int32), axis=0)
        sorted_rows = jnp.take(recv_rows.reshape(dev_count * row_cap, model_dim), sort_order, axis=0)
        out_sorted = expert_ffn(sorted_rows, group_sizes, w_one, w_three, w_two)
        out_rows = jnp.take(out_sorted, jnp.argsort(sort_order), axis=0)
        back_rows = lax.all_to_all(out_rows.reshape(dev_count, row_cap, model_dim), "ep", 0, 0, tiled=True)
        picked_rows = jnp.take(back_rows.reshape(dev_count * row_cap, model_dim), slot_pos, axis=0)
        both_out = picked_rows.reshape(tok_count, 2, model_dim).astype(jnp.float32)
        return jnp.sum(gate_vals[:, :, None] * both_out, axis=1).astype(jnp.bfloat16)

    return jax.shard_map(device_body, mesh=mesh, in_specs=(P("ep", None), P(None, None), P("ep", None), P("ep", None, None), P("ep", None, None), P("ep", None, None)), out_specs=P("ep", None), check_vma=False)
```

profile of v0, /device:TPU:27, one launch (start us, length us, event | category | flops | bytes accessed | tf_op | source)
XLA Modules:
  0.0 1325.8 jit_solution(9483355350381554567)
XLA Ops:
  0.0 1.1 copy.37
  2.1 0.7 broadcast_multiply_fusion
  2.8 9.2 reduce-window.6
  12.1 0.8 slice_reduce_fusion
  14.7 16.1 %scatter_custom_fusion.1 = s32[8192]{0:T(1024)} fusion(s32[4096]{0:T(1024)S(1)} %bitcast.35, s32[4096]{0:T(1024)S(1)} %broadcast.172, s32[]{:T(128)} %constant.110.clone.1), kind=kCustom, calls=%fused_computation.49 | custom fusion | bytes 32772 | tf_op jit(solution)/shard_map/scatter | solution.py:37
  30.8 6.1 all-to-all-start.1
  37.0 15.5 %scatter_custom_fusion = s32[8192]{0:T(1024)S(1)} fusion(s32[4096]{0:T(1024)S(1)} %bitcast.36, s32[4096]{0:T(1024)S(1)} %add_select_fusion, s32[]{:T(128)} %constant.100.clone.1), kind=kCustom, calls=%fused_computation.47 | custom fusion | bytes 32772 | tf_op jit(solution)/shard_map/scatter | solution.py:36
  52.6 43.4 %gather_fusion = bf16[8192,1024]{1,0:T(8,128)(2,1)} fusion(bf16[2048,1024]{1,0:T(8,128)(2,1)} %param.8, s32[8192]{0:T(1024)S(1)} %fusion.5), kind=kCustom, calls=%fused_computation.2 | custom fusion | bytes 33587200 | tf_op jit(solution)/shard_map/jit(_take)/gather | solution.py:38
  96.0 14.2 %broadcast_select_fusion.2 = bf16[32,256,1024]{2,1,0:T(8,128)(2,1)} fusion(bf16[32,256,1024]{2,1,0:T(8,128)(2,1)} %bitcast.29, pred[32,256]{1,0:T(8,128)(4,1)S(1)} %broadcast_in_dim.54), kind=kLoop, calls=%fused_computation.11 | loop fusion | flops 8388608 | bytes 33562624 | tf_op jit(solution)/shard_map/jit(_take)/select_n | solution.py:38
  110.2 5.9 all-to-all-start
  116.7 1.6 ragged-dot-metadata
  118.4 6.8 sort.34
  125.1 6.8 sort.35
  133.2 346.2 %all-to-all-done = bf16[32,256,1024]{2,1,0:T(8,128)(2,1)} async-done(((bf16[32,256,1024]{2,1,0:T(8,128)(2,1)}), bf16[32,256,1024]{2,1,0:T(8,128)(2,1)}, u32[]{:S(2)}, u32[]{:S(2)}) %all-to-all-start) | async-done | bytes 16777248 | tf_op jit(solution)/shard_map/all_to_all | solution.py:39
  479.3 48.5 %gather_fusion.3 = bf16[8192,1024]{1,0:T(8,128)(2,1)} fusion(bf16[8192,1024]{1,0:T(8,128)(2,1)} %bitcast.8, s32[8192]{0:T(1024)S(1)} %fusion.6), kind=kCustom, calls=%fused_computation.clone | custom fusion | bytes 33587200 | tf_op jit(solution)/shard_map/jit(_take)/gather | solution.py:44
  527.9 14.2 %broadcast_select_fusion.1 = bf16[8192,1024]{1,0:T(8,128)(2,1)} fusion(bf16[8192,1024]{1,0:T(8,128)(2,1)} %gather_fusion.3, pred[8192]{0:T(1024)(128)(4,1)S(1)} %compare_and_fusion.1), kind=kLoop, calls=%fused_computation.10 | loop fusion | flops 8388608 | bytes 33562624 | tf_op jit(solution)/shard_map/jit(_take)/select_n | solution.py:44
  542.0 24.9 %ragged-dot-none.2 = f32[8192,2816]{1,0:T(8,128)} custom-call(s32[1]{0:T(128)} %get-tuple-element.10, s32[2]{0:T(128)} %get-tuple-element.11, s32[32]{0:T(128)} %get-tuple-element.12, s32[32]{0:T(128)} %get-tuple-element.13, s32[1]{0:T(128)} %get-tuple-element.10, bf16[8192,1024]{1,0:T(8,128)(2,1)} %broadcast_select_fusion.1, bf16[1,1024,2816]{2,1,0:T(8,128)(2,1)} %param.11), custom_call_target="tpu_custom_call" | custom-call | flops 47244640256 | bytes 114819072 | tf_op jit(solution)/shard_map/ragged_dot_general/ragged-dot-none
  566.9 25.2 %ragged-dot-none.1 = f32[8192,2816]{1,0:T(8,128)} custom-call(s32[1]{0:T(128)} %get-tuple-element.10, s32[2]{0:T(128)} %get-tuple-element.11, s32[32]{0:T(128)} %get-tuple-element.12, s32[32]{0:T(128)} %get-tuple-element.13, s32[1]{0:T(128)} %get-tuple-element.10, bf16[8192,1024]{1,0:T(8,128)(2,1)} %broadcast_select_fusion.1, bf16[1,1024,2816]{2,1,0:T(8,128)(2,1)} %param.12), custom_call_target="tpu_custom_call" | custom-call | flops 47244640256 | bytes 114819072 | tf_op jit(solution)/shard_map/ragged_dot_general/ragged-dot-none
  592.0 72.3 %multiply_convert_fusion = bf16[8192,2816]{1,0:T(8,128)(2,1)} fusion(f32[8192,2816]{1,0:T(8,128)} %ragged-dot-none.1, f32[8192,2816]{1,0:T(8,128)} %ragged-dot-none.2), kind=kLoop, calls=%fused_computation.7 | loop fusion | flops 138412032 | bytes 230686720 | tf_op jit(solution)/shard_map/convert_element_type | solution.py:17
  664.3 24.6 %ragged-dot-none = f32[8192,1024]{1,0:T(8,128)} custom-call(s32[1]{0:T(128)} %get-tuple-element.10, s32[2]{0:T(128)} %get-tuple-element.11, s32[32]{0:T(128)} %get-tuple-element.12, s32[32]{0:T(128)} %get-tuple-element.13, s32[1]{0:T(128)} %get-tuple-element.10, bf16[8192,2816]{1,0:T(8,128)(2,1)} %multiply_convert_fusion, bf16[1,2816,1024]{2,1,0:T(8,128)(2,1)} %param.13), custom_call_target="tpu_custom_call" | custom-call | flops 47244640256 | bytes 85458944 | tf_op jit(solution)/shard_map/ragged_dot_general/ragged-dot-none
  689.0 17.5 %convert_element_type.28 = bf16[8192,1024]{1,0:T(8,128)(2,1)} convert(f32[8192,1024]{1,0:T(8,128)} %ragged-dot-none) | non-fusion elementwise | flops 8388608 | bytes 50331648 | tf_op jit(solution)/shard_map/convert_element_type | solution.py:18
  706.5 48.6 %gather_fusion.4 = bf16[8192,1024]{1,0:T(8,128)(2,1)} fusion(bf16[8192,1024]{1,0:T(8,128)(2,1)} %convert_element_type.28, s32[8192]{0:T(1024)S(1)} %copy-done.7), kind=kCustom, calls=%fused_computation.1.clone | custom fusion | bytes 33587200 | tf_op jit(solution)/shard_map/jit(_take)/gather | solution.py:46
  755.1 14.2 %broadcast_select_fusion = bf16[8192,1024]{1,0:T(8,128)(2,1)} fusion(bf16[8192,1024]{1,0:T(8,128)(2,1)} %gather_fusion.4, pred[8192]{0:T(1024)(128)(4,1)S(1)} %copy-done.10), kind=kLoop, calls=%fused_computation.9 | loop fusion | flops 8388608 | bytes 33562624 | tf_op jit(solution)/shard_map/jit(_take)/select_n | solution.py:46
  769.3 112.2 %all-to-all-start.2 = ((bf16[32,256,1024]{2,1,0:T(8,128)(2,1)}), bf16[32,256,1024]{2,1,0:T(8,128)(2,1)}, u32[]{:S(2)}, u32[]{:S(2)}) async-start(bf16[32,256,1024]{2,1,0:T(8,128)(2,1)} %bitcast.30), calls=%async_computation.2 | async-start | bytes 33554432 | tf_op jit(solution)/shard_map/all_to_all | solution.py:47
  881.4 2.0 sub.27
  884.3 3.5 fusion.16
  888.0 33.0 %gather_fusion.2 = f32[4096]{0:T(1024)S(1)} fusion(f32[2048,32]{0,1:T(8,128)S(1)} %fusion.3, s32[4096]{0:T(1024)S(1)} %reshape.171), kind=kCustom, calls=%fused_computation.4 | custom fusion | bytes 65536 | tf_op jit(solution)/shard_map/jit(take_along_axis)/gather | solution.py:10
  921.1 1.0 reshape.174
  923.7 320.5 %all-to-all-done.2 = bf16[32,256,1024]{2,1,0:T(8,128)(2,1)} async-done(((bf16[32,256,1024]{2,1,0:T(8,128)(2,1)}), bf16[32,256,1024]{2,1,0:T(8,128)(2,1)}, u32[]{:S(2)}, u32[]{:S(2)}) %all-to-all-start.2) | async-done | bytes 16777248 | tf_op jit(solution)/shard_map/all_to_all | solution.py:47
  1244.2 28.9 %gather_fusion.1 = bf16[4096,1024]{1,0:T(8,128)(2,1)} fusion(bf16[8192,1024]{1,0:T(8,128)(2,1)} %bitcast.10, s32[4096]{0:T(1024)S(1)} %broadcast_clamp_fusion), kind=kCustom, calls=%fused_computation.3 | custom fusion | bytes 16793600 | tf_op jit(solution)/shard_map/jit(_take)/gather | solution.py:48
  1273.1 13.1 gather.23
  1286.2 39.2 %multiply_reduce_fusion = bf16[2048,1024]{1,0:T(8,128)(2,1)} fusion(bf16[2048,2,1024]{2,1,0:T(2,128)(2,1)} %gather.23, pred[2048,2]{1,0:T(8,128)(4,1)S(1)} %copy.40, f32[2048,2]{1,0:T(8,128)S(1)} %copy.36), kind=kLoop, calls=%fused_computation.8 | loop fusion | flops 14680064 | bytes 12603392 | tf_op jit(solution)/shard_map/reduce_sum | solution.py:50
  (58 shorter events, 7.3 us)
Async XLA Ops:
  0.0 884.3 %copy-start = (f32[1024,32]{0,1:T(8,128)S(1)}, f32[1024,32]{0,1:T(8,128)}, u32[]{:S(2)}) copy-start(f32[1024,32]{0,1:T(8,128)} %param.9) | copy-start | bytes 393220
  13.6 82.4 %copy-start.5 = (s32[4096]{0:T(1024)}, s32[4096]{0:T(1024)S(1)}, u32[]{:S(2)}) copy-start(s32[4096]{0:T(1024)S(1)} %broadcast_add_fusion.1) | copy-start | bytes 49156
  14.7 22.3 %copy-start.8 = (s32[4096,1]{0,1:T(1,128)}, s32[4096,1]{0,1:T(1,128)S(1)}, u32[]{:S(2)}) copy-start(s32[4096,1]{0,1:T(1,128)S(1)} %compare_select_fusion) | copy-start | bytes 49156
  30.8 79.4 %all-to-all-start.1 = ((s32[32,1,256]{2,1,0:T(1,128)}), s32[32,1,256]{2,1,0:T(1,128)S(1)}, u32[]{:S(2)}, u32[]{:S(2)}) async-start(s32[32,1,256]{2,1,0:T(1,128)} %bitcast.4), calls=%async_computation.1 | async-start | bytes 65536 | tf_op jit(solution)/shard_map/all_to_all | solution.py:40
  110.2 369.1 %all-to-all-start = ((bf16[32,256,1024]{2,1,0:T(8,128)(2,1)}), bf16[32,256,1024]{2,1,0:T(8,128)(2,1)}, u32[]{:S(2)}, u32[]{:S(2)}) async-start(bf16[32,256,1024]{2,1,0:T(8,128)(2,1)} %broadcast_select_fusion.2), calls=%async_computation | async-start | bytes 33554432 | tf_op jit(solution)/shard_map/all_to_all | solution.py:39
  688.9 17.5 %copy-start.7 = (s32[8192]{0:T(1024)S(1)}, s32[8192]{0:T(1024)}, u32[]{:S(2)}) copy-start(s32[8192]{0:T(1024)} %fusion.7) | copy-start | bytes 98308
  706.5 48.6 %copy-start.10 = (pred[8192]{0:T(1024)(128)(4,1)S(1)}, pred[8192]{0:T(1024)(128)(4,1)}, u32[]{:S(2)}) copy-start(pred[8192]{0:T(1024)(128)(4,1)} %compare_and_fusion) | copy-start | bytes 24580
  769.3 112.2 %copy-start.6 = (s32[4096]{0:T(1024)S(1)}, s32[4096]{0:T(1024)}, u32[]{:S(2)}) copy-start(s32[4096]{0:T(1024)} %copy-done.5) | copy-start | bytes 49156
  769.3 114.2 %copy-start.3 = (s32[2048,2]{0,1:T(2,128)S(1)}, s32[2048,2]{0,1:T(2,128)}, u32[]{:S(2)}) copy-start(s32[2048,2]{0,1:T(2,128)} %param.10) | copy-start | bytes 49156
  769.3 474.9 %all-to-all-start.2 = ((bf16[32,256,1024]{2,1,0:T(8,128)(2,1)}), bf16[32,256,1024]{2,1,0:T(8,128)(2,1)}, u32[]{:S(2)}, u32[]{:S(2)}) async-start(bf16[32,256,1024]{2,1,0:T(8,128)(2,1)} %bitcast.30), calls=%async_computation.2 | async-start | bytes 33554432 | tf_op jit(solution)/shard_map/all_to_all | solution.py:47
  888.0 34.4 %copy-start.4 = (s32[2048,2]{0,1:T(2,128)S(1)}, s32[2048,2]{0,1:T(2,128)}, u32[]{:S(2)}) copy-start(s32[2048,2]{0,1:T(2,128)} %param.10) | copy-start | bytes 49156
  888.0 34.9 %copy-start.2 = (s32[2048,2]{1,0:T(8,128)S(1)}, s32[2048,2]{1,0:T(8,128)}, u32[]{:S(2)}) copy-start(s32[2048,2]{1,0:T(8,128)} %sub.27) | copy-start | bytes 49156
  888.0 35.7 %copy-start.9 = (s32[4096,1]{0,1:T(1,128)S(1)}, s32[4096,1]{0,1:T(1,128)}, u32[]{:S(2)}) copy-start(s32[4096,1]{0,1:T(1,128)} %copy-done.8) | copy-start | bytes 49156
  1244.2 81.2 %copy-start.1 = (f32[1024,32]{0,1:T(8,128)S(1)}, f32[1024,32]{0,1:T(8,128)}, u32[]{:S(2)}) copy-start(f32[1024,32]{0,1:T(8,128)} %param.9) | copy-start | bytes 393220
where the time goes:
time: 1340 us; the launch traced here: 1330 us
  waiting for transfers between devices  667 us (50%)
  local copies, waits for them, and re-layouts  256 us (19%)
  other arithmetic  198 us (15%)
  starting transfers between devices  124 us (9%)
  Pallas kernels  76.3 us (6%)
    all_to_all x1, waiting for transfers between devices, device_body(): recv_rows = lax.all_to_all(send_rows, 'ep', 0, 0, tiled=True)  346 us
    all_to_all x1, waiting for transfers between devices, device_body(): lax.all_to_all(out_rows.reshape(dev_count, row_cap, model_dim), 'ep', 0,...  320 us
    all_to_all x1, starting transfers between devices, device_body(): lax.all_to_all(out_rows.reshape(dev_count, row_cap, model_dim), 'ep', 0,...  112 us
    another operation x3, Pallas kernels  74.7 us
    convert_element_type x1, other arithmetic, expert_ffn(): act_rows = (jax.nn.silu(h_one) * h_three).astype(jnp.bfloat16)  72.3 us
    gather x1, local copies, waits for them, and re-layouts, device_body(): out_rows = jnp.take(out_sorted, jnp.argsort(sort_order), axis=0)  48.6 us
    gather x1, local copies, waits for them, and re-layouts, device_body(): jnp.take(recv_rows.reshape(dev_count * row_cap, model_dim), sort_order, a...  48.5 us
    gather x1, local copies, waits for them, and re-layouts, device_body(): jnp.take(hidden_loc, src_token, axis=0)  43.4 us
  transfers between devices with their start and end apart: 3, of which 2 were waited for; matrix products, arithmetic and copies ran while one was open for 10% of the time, Pallas kernels for 0%

commit v1 on v0

v1 whole, which is shorter than its diff:
```python
import functools

import jax
import jax.numpy as jnp
from jax import lax
from jax.experimental import pallas as pl
from jax.experimental.pallas import tpu as pltpu
from jax.sharding import PartitionSpec as P

MESH = pl.DeviceIdType.MESH
NZ = 4
NQ = 8
HALVES = 2


def moe_kernel(hid_hbm, ids_ref, w1_hbm, w3_hbm, w2_hbm, back_hbm, pos_ref,
               hid, send, recv, w1, w3, w2, act, sel, rank, rank_in,
               own_sem, w_sem, z_send, z_recv, r_send, r_recv,
               p_send, p_recv, b_send, b_recv, loc_sem):
    me = lax.axis_index("ep")
    z = me // NQ
    q = me % NQ
    mirror = z // 2
    zz = z + mirror * (3 - 2 * z)
    tok = hid_hbm.shape[0]
    dim = hid_hbm.shape[1]
    ff = w1.shape[1]
    cap = back_hbm.shape[1]
    half_tok = tok // HALVES
    pair = 2 * cap
    nt = min(256, dim)
    ft = min(256, ff)

    def block_of(step):
        near = (0, 1, 2, 3)[step]
        inner = (1, 2, 0, 3)[step]
        pick = near + zz * (inner - near)
        return pick + mirror * (3 - 2 * pick)

    def half(ref, h):
        return ref.at[pl.ds(h * half_tok, half_tok)]

    def z_copy(direction, hop, h, block, src=None):
        target = me + (NQ if direction == 0 else -NQ)
        return pltpu.make_async_remote_copy(
            src_ref=half(hid.at[block] if src is None else src, h),
            dst_ref=half(hid.at[block], h),
            send_sem=z_send.at[direction, hop - 1, h],
            recv_sem=z_recv.at[direction, hop - 1, h],
            device_id=(target,), device_id_type=MESH)

    def rank_copy(plane):
        return pltpu.make_async_remote_copy(
            src_ref=rank.at[plane], dst_ref=rank_in.at[z],
            send_sem=r_send.at[plane], recv_sem=r_recv.at[z],
            device_id=(plane * NQ + q,), device_id_type=MESH)

    def plane_copy(step, peer):
        return pltpu.make_async_remote_copy(
            src_ref=send.at[pl.ds(peer * cap, cap)],
            dst_ref=recv.at[step, pl.ds(q * cap, cap)],
            send_sem=p_send.at[peer], recv_sem=p_recv.at[step, q],
            device_id=(z * NQ + peer,), device_id_type=MESH)

    def plane_arrival(step, peer):
        return pltpu.make_async_remote_copy(
            src_ref=send.at[pl.ds(peer * cap, cap)],
            dst_ref=recv.at[step, pl.ds(peer * cap, cap)],
            send_sem=p_send.at[peer], recv_sem=p_recv.at[step, peer],
            device_id=(z * NQ + peer,), device_id_type=MESH)

    def back_copy(step, peer):
        return pltpu.make_async_remote_copy(
            src_ref=recv.at[step, pl.ds(peer * cap, cap)],
            dst_ref=back_hbm.at[me],
            send_sem=b_send.at[step, peer], recv_sem=b_recv.at[me],
            device_id=(block_of(step) * NQ + peer,), device_id_type=MESH)

    own_load = pltpu.make_async_copy(hid_hbm, hid.at[z], own_sem)
    for h in range(HALVES):
        @pl.when(z < NZ - 1)
        def _():
            z_copy(0, 1, h, z, hid_hbm).start()

        @pl.when(z > 0)
        def _():
            z_copy(1, 1, h, z, hid_hbm).start()
    own_load.start()
    w_loads = [pltpu.make_async_copy(src, dst, w_sem.at[k])
               for k, (src, dst) in enumerate(((w1_hbm, w1), (w3_hbm, w3), (w2_hbm, w2)))]
    for load in w_loads:
        load.start()

    n_exp = NZ * NQ
    lanes = min(256, tok)
    exp_iota = lax.broadcasted_iota(jnp.int32, (n_exp, lanes), 0)
    row_iota = lax.broadcasted_iota(jnp.int32, (lanes, lanes), 0)
    col_iota = lax.broadcasted_iota(jnp.int32, (lanes, lanes), 1)
    below = (row_iota < col_iota).astype(jnp.float32).astype(jnp.bfloat16)
    carry = jnp.zeros((n_exp, 1), jnp.float32)
    for k in range(tok // lanes):
        span = pl.ds(k * lanes, lanes)
        first = ids_ref[pl.ds(0, 1), span] == exp_iota
        second = ids_ref[pl.ds(1, 1), span] == exp_iota
        chosen = jnp.where(first, 1.0, 0.0) + jnp.where(second, 1.0, 0.0)
        count = jnp.dot(chosen.astype(jnp.bfloat16), below, preferred_element_type=jnp.float32) + carry
        carry = carry + jnp.sum(chosen, axis=1, keepdims=True)
        marked = jnp.where(chosen > 0.5, count, -1.0)
        for plane in range(NZ):
            rank[plane, :, span] = marked[plane * NQ:(plane + 1) * NQ]
        slot0 = jnp.sum(jnp.where(first, count, 0.0), axis=0, keepdims=True).astype(jnp.int32)
        slot1 = jnp.sum(jnp.where(second, count, 0.0), axis=0, keepdims=True).astype(jnp.int32)
        pos_ref[pl.ds(0, 1), span] = ids_ref[pl.ds(0, 1), span] * cap + slot0
        pos_ref[pl.ds(1, 1), span] = ids_ref[pl.ds(1, 1), span] * cap + slot1
    for plane in range(NZ):
        @pl.when(z != plane)
        def _():
            rank_copy(plane).start()

        @pl.when(z == plane)
        def _():
            rank_in[plane] = rank[plane]

    def relay(hop, h):
        @pl.when(z >= hop)
        def _():
            z_copy(0, hop, h, z - hop).wait_recv()

        @pl.when(jnp.logical_and(z >= hop, z < NZ - 1))
        def _():
            z_copy(0, hop + 1, h, z - hop).start()

        @pl.when(z + hop < NZ)
        def _():
            z_copy(1, hop, h, z + hop).wait_recv()

        @pl.when(jnp.logical_and(z + hop < NZ, z > 0))
        def _():
            z_copy(1, hop + 1, h, z + hop).start()

    def select(step):
        block = block_of(step)
        if step > 0:
            pltpu.make_async_remote_copy(
                src_ref=rank.at[0], dst_ref=rank_in.at[block],
                send_sem=r_send.at[block], recv_sem=r_recv.at[block],
                device_id=(block * NQ + q,), device_id_type=MESH).wait_recv()
        slot_iota = lax.broadcasted_iota(jnp.int32, (cap, tok), 0).astype(jnp.float32)

        @pl.loop(0, NQ // 2)
        def _(k):
            p = (q // 2 + 1 + k) % (NQ // 2)
            for j in range(2):
                peer = 2 * p + j
                if step > 0:
                    @pl.when(peer != q)
                    def _():
                        plane_copy(step - 1, peer).wait_send()
                row = rank_in[block, pl.ds(peer, 1), :]
                sel[pl.ds(j * cap, cap), :] = jnp.where(slot_iota == row, 1.0, 0.0).astype(jnp.bfloat16)

            @pl.loop(0, dim // nt)
            def _(n):
                cols = pl.ds(pl.multiple_of(n * nt, nt), nt)
                send[pl.ds(p * pair, pair), cols] = jnp.dot(
                    sel[...], hid[block, :, cols], preferred_element_type=jnp.float32).astype(jnp.bfloat16)

            for j in range(2):
                peer = 2 * p + j

                @pl.when(peer != q)
                def _():
                    plane_copy(step, peer).start()

                @pl.when(peer == q)
                def _():
                    recv[step, pl.ds(peer * cap, cap), :] = send[pl.ds(peer * cap, cap), :]

    def experts(step):
        block = block_of(step)

        @pl.loop(0, NQ // 2)
        def _(k):
            p = (q // 2 + NQ // 2 - k) % (NQ // 2)
            for j in range(2):
                peer = 2 * p + j

                @pl.when(peer != q)
                def _():
                    plane_arrival(step, peer).wait_recv()
            rows = pl.ds(p * pair, pair)

            @pl.loop(0, ff // ft)
            def _(f):
                cols = pl.ds(pl.multiple_of(f * ft, ft), ft)
                x = recv[step, rows, :]
                u = jnp.dot(x, w1[:, cols], preferred_element_type=jnp.float32)
                v = jnp.dot(x, w3[:, cols], preferred_element_type=jnp.float32)
                act[:, cols] = (jax.nn.silu(u) * v).astype(jnp.bfloat16)

            @pl.loop(0, dim // nt)
            def _(n):
                cols = pl.ds(pl.multiple_of(n * nt, nt), nt)
                recv[step, rows, cols] = jnp.dot(
                    act[...], w2[:, cols], preferred_element_type=jnp.float32).astype(jnp.bfloat16)

            for j in range(2):
                peer = 2 * p + j
                home = block * NQ + peer

                @pl.when(home != me)
                def _():
                    back_copy(step, peer).start()

                @pl.when(home == me)
                def _():
                    pltpu.make_async_copy(recv.at[step, pl.ds(peer * cap, cap)], back_hbm.at[me], loc_sem).start()

    own_load.wait()
    select(0)
    relay(1, 0)
    relay(1, 1)
    select(1)
    for load in w_loads:
        load.wait()
    experts(0)
    relay(2, 0)

    @pl.when(zz == 0)
    def _():
        relay(2, 1)
    select(2)
    experts(1)

    @pl.when(zz == 1)
    def _():
        relay(2, 1)
    for h in range(HALVES):
        @pl.when(z >= 3)
        def _():
            z_copy(0, 3, h, z - 3).wait_recv()

        @pl.when(z + 3 < NZ)
        def _():
            z_copy(1, 3, h, z + 3).wait_recv()
    select(3)
    experts(2)
    experts(3)

    for h in range(HALVES):
        for hop in range(1, NZ):
            @pl.when(jnp.logical_and(z < NZ - 1, z >= hop - 1))
            def _():
                z_copy(0, hop, h, z - (hop - 1)).wait_send()

            @pl.when(jnp.logical_and(z > 0, z + (hop - 1) < NZ))
            def _():
                z_copy(1, hop, h, z + (hop - 1)).wait_send()
    for plane in range(NZ):
        @pl.when(z != plane)
        def _():
            rank_copy(plane).wait_send()

    @pl.loop(0, NQ)
    def _(peer):
        @pl.when(peer != q)
        def _():
            plane_copy(NZ - 1, peer).wait_send()
        for step in range(NZ):
            @pl.when(block_of(step) * NQ + peer != me)
            def _():
                back_copy(step, peer).wait_send()
    pltpu.make_async_copy(recv.at[0, pl.ds(q * cap, cap)], back_hbm.at[me], loc_sem).wait()

    @pl.loop(1, NZ * NQ)
    def _(k):
        other = (me + k) % (NZ * NQ)
        pltpu.make_async_remote_copy(
            src_ref=recv.at[0, pl.ds(0, cap)], dst_ref=back_hbm.at[other],
            send_sem=b_send.at[0, 0], recv_sem=b_recv.at[other],
            device_id=(other,), device_id_type=MESH).wait_recv()


def moe_exchange(hidden_loc, ids_t, w_one, w_three, w_two, n):
    tok, dim = hidden_loc.shape
    ff = w_one.shape[1]
    cap = 4 * tok // n
    any_spec = pl.BlockSpec(memory_space=pl.ANY)
    vmem_spec = pl.BlockSpec(memory_space=pltpu.VMEM)
    dma = pltpu.SemaphoreType.DMA
    rows = n * cap
    flops = 2 * rows * (3 * dim * ff + tok * dim)
    return pl.pallas_call(
        moe_kernel,
        out_shape=(jax.ShapeDtypeStruct((n, cap, dim), jnp.bfloat16),
                   jax.ShapeDtypeStruct((2, tok), jnp.int32)),
        in_specs=[any_spec, vmem_spec, any_spec, any_spec, any_spec],
        out_specs=(any_spec, vmem_spec),
        scratch_shapes=[
            pltpu.VMEM((NZ, tok, dim), jnp.bfloat16),
            pltpu.VMEM((NQ * cap, dim), jnp.bfloat16),
            pltpu.VMEM((NZ, NQ * cap, dim), jnp.bfloat16),
            pltpu.VMEM((dim, ff), jnp.bfloat16),
            pltpu.VMEM((dim, ff), jnp.bfloat16),
            pltpu.VMEM((ff, dim), jnp.bfloat16),
            pltpu.VMEM((2 * cap, ff), jnp.bfloat16),
            pltpu.VMEM((2 * cap, tok), jnp.bfloat16),
            pltpu.VMEM((NZ, NQ, tok), jnp.float32),
            pltpu.VMEM((NZ, NQ, tok), jnp.float32),
            dma(()), dma((3,)), dma((2, NZ - 1, HALVES)), dma((2, NZ - 1, HALVES)),
            dma((NZ,)), dma((NZ,)), dma((NQ,)), dma((NZ, NQ)),
            dma((NZ, NQ)), dma((NZ * NQ,)), dma(()),
        ],
        compiler_params=pltpu.CompilerParams(has_side_effects=True, vmem_limit_bytes=67043328),
        cost_estimate=pl.CostEstimate(flops=flops, bytes_accessed=2 * rows * dim * 4, transcendentals=rows * ff),
    )(hidden_loc, ids_t, w_one, w_three, w_two)


def route_gates(hidden_loc, w_router, ids_loc):
    logits = jnp.dot(hidden_loc.astype(jnp.float32), w_router, preferred_element_type=jnp.float32)
    prob_vals = jax.nn.softmax(logits, axis=-1)
    exp_iota = lax.broadcasted_iota(jnp.int32, prob_vals.shape, 1)
    p_a = jnp.sum(jnp.where(exp_iota == ids_loc[:, 0:1], prob_vals, 0.0), axis=1, keepdims=True)
    p_b = jnp.sum(jnp.where(exp_iota == ids_loc[:, 1:2], prob_vals, 0.0), axis=1, keepdims=True)
    total = p_a + p_b
    return p_a / total, p_b / total


def solution(mesh):
    n = mesh.shape["ep"]

    def device_body(hidden_loc, w_router, ids_loc, w_one, w_three, w_two):
        dim = hidden_loc.shape[1]
        back, pos = moe_exchange(hidden_loc, ids_loc.T, w_one[0], w_three[0], w_two[0], n)
        flat = back.reshape(-1, dim)
        g_a, g_b = route_gates(hidden_loc, w_router, ids_loc)
        e_a = jnp.take(flat, pos[0], axis=0, mode="clip").astype(jnp.float32)
        e_b = jnp.take(flat, pos[1], axis=0, mode="clip").astype(jnp.float32)
        return (g_a * e_a + g_b * e_b).astype(jnp.bfloat16)

    return jax.shard_map(device_body, mesh=mesh, in_specs=(P("ep", None), P(None, None), P("ep", None), P("ep", None, None), P("ep", None, None), P("ep", None, None)), out_specs=P("ep", None), check_vma=False)
```

time: 1340 us -> 733 us (0.55); the launches traced: 1330 us -> 733 us
  waiting for transfers between devices: 667 us -> 0 us
  Pallas kernels: 76.3 us -> 686 us
  local copies, waits for them, and re-layouts: 256 us -> 38.8 us
  other arithmetic: 198 us -> 4.76 us
  starting transfers between devices: 124 us -> 0 us
    pallas_call x0 -> x1, Pallas kernels: none -> 686 us  [moe_exchange(): pl.pallas_call(moe_kernel, out_shape=(jax.ShapeDtypeStruct((n, cap, dim),...]
    all_to_all x3 -> x0, waiting for transfers between devices: 667 us -> none  [the longest x1 346 us: device_body(): recv_rows = lax.all_to_all(send_rows, 'ep', 0, 0, tiled=True)]
    gather x10 -> x2, local copies, waits for them, and re-layouts: 218 us -> 38 us  [the longest x1 19 us: device_body(): e_b = jnp.take(flat, pos[1], axis=0, mode='clip').astype(jnp.float32)]
    all_to_all x3 -> x0, starting transfers between devices: 124 us -> none  [the longest x1 112 us: device_body(): lax.all_to_all(out_rows.reshape(dev_count, row_cap, model_dim), 'ep', 0,...]
    convert_element_type x3 -> x1, other arithmetic: 89.9 us -> 4.56 us  [device_body(): return (g_a * e_a + g_b * e_b).astype(jnp.bfloat16)]
    another operation x3 -> x0, Pallas kernels: 74.7 us -> none
    select_n x5 -> x0, other arithmetic: 42.6 us -> none  [the longest x1 14.2 us: device_body(): jnp.take(hidden_loc, src_token, axis=0)]
    reduce_sum x4 -> x1, other arithmetic: 40.3 us -> 0.13 us  [route_gates(): jnp.sum(jnp.where(exp_iota == ids_loc[:, 0:1], prob_vals, 0.0), axis=1, k...]
  transfers between devices with their start and end apart: 3 -> 0, of which waited for: 2 -> 0; matrix products, arithmetic and copies ran while one was open for 10% -> 0% of each run, Pallas kernels for 0% -> 0%
where the time goes in v1:
time: 733 us
  Pallas kernels  686 us (94%)
  local copies, waits for them, and re-layouts  38.8 us (5%)
    pallas_call x1, Pallas kernels, moe_exchange(): pl.pallas_call(moe_kernel, out_shape=(jax.ShapeDtypeStruct((n, cap, dim),...  686 us
    gather x1, local copies, waits for them, and re-layouts, device_body(): e_b = jnp.take(flat, pos[1], axis=0, mode='clip').astype(jnp.float32)  19 us
    gather x1, local copies, waits for them, and re-layouts, device_body(): e_a = jnp.take(flat, pos[0], axis=0, mode='clip').astype(jnp.float32)  19 us

profile of v1, /device:TPU:27, one launch (start us, length us, event | category | flops | bytes accessed | tf_op | source)
XLA Modules:
  0.0 733.0 jit_solution(14803954218678653545)
XLA Ops:
  0.0 685.7 %shard_map.64 = (bf16[32,256,1024]{2,1,0:T(8,128)(2,1)}, s32[2,2048]{1,0:T(2,128)}) custom-call(bf16[2048,1024]{1,0:T(8,128)(2,1)} %hid_hbm.1, s32[2,2048]{1,0:T(2,128)} %bitcast.17, bf16[1024,2816]{1,0:T(8,128)(2,1)} %bitcast.18, bf16[1024,2816]{1,0:T(8,128)(2,1)} %bitcast.19, bf16[2816,1024]{1,0:T(8,128)(2,1)} %bitcast.20), custom_call_target="tpu_custom_call" | custom-call | flops 176093659136 | bytes 67108864 | tf_op jit(solution)/shard_map/pallas_call | solution.py:293
  685.7 0.8 fusion.3
  686.5 19.0 %gather_fusion.1 = bf16[2048,1024]{1,0:T(8,128)(2,1)} fusion(bf16[8192,1024]{1,0:T(8,128)(2,1)} %bitcast.11, s32[2048]{0:T(1024)S(1)} %broadcast_clamp_fusion), kind=kCustom, calls=%fused_computation.1 | custom fusion | bytes 8396800 | tf_op jit(solution)/shard_map/jit(_take)/gather | solution.py:338
  705.5 0.0 copy-start.2
  705.5 0.0 copy-start.1
  705.5 19.0 %gather_fusion = bf16[2048,1024]{1,0:T(8,128)(2,1)} fusion(bf16[8192,1024]{1,0:T(8,128)(2,1)} %bitcast.12, s32[2048]{0:T(1024)S(1)} %broadcast_clamp_fusion.1), kind=kCustom, calls=%fused_computation | custom fusion | bytes 8396800 | tf_op jit(solution)/shard_map/jit(_take)/gather | solution.py:337
  724.5 0.0 copy-done.2
  724.5 0.0 copy-start
  724.5 0.0 copy-done.1
  724.5 3.7 fusion.4
  728.2 0.1 fusion.1
  728.3 0.1 select_reduce_fusion.1
  728.4 0.0 copy-done
  728.5 4.6 add_convert_fusion
  (4 shorter events, 0.0 us)
Async XLA Ops:
  705.5 19.0 %copy-start.2 = (s32[2048,2]{0,1:T(2,128)S(1)}, s32[2048,2]{0,1:T(2,128)}, u32[]{:S(2)}) copy-start(s32[2048,2]{0,1:T(2,128)} %param.8) | copy-start | bytes 49156
  705.5 19.0 %copy-start.1 = (f32[1024,32]{0,1:T(8,128)S(1)}, f32[1024,32]{0,1:T(8,128)}, u32[]{:S(2)}) copy-start(f32[1024,32]{0,1:T(8,128)} %param.7) | copy-start | bytes 393220
  724.5 3.9 copy-start

commit v2 on v1

--- a/solution.py
+++ b/solution.py
@@ -11,12 +11,13 @@
 NZ = 4
 NQ = 8
 HALVES = 2
-
-
-def moe_kernel(hid_hbm, ids_ref, w1_hbm, w3_hbm, w2_hbm, back_hbm, pos_ref,
-               hid, send, recv, w1, w3, w2, act, sel, rank, rank_in,
+PIECES = 4
+
+
+def moe_kernel(limit, cap, hid_hbm, ids_ref, w1_hbm, w3_hbm, w2_hbm, rows_hbm, land_hbm, pos_ref,
+               hid, send, recv, w1, w3, w2, act, sel, rank, rank_in, slots,
                own_sem, w_sem, z_send, z_recv, r_send, r_recv,
-               p_send, p_recv, b_send, b_recv, loc_sem):
+               p_send, p_recv, l_send, l_recv, loc_sem, stage_sem, b_send, b_recv):
     me = lax.axis_index("ep")
     z = me // NQ
     q = me % NQ
@@ -25,7 +26,8 @@
     tok = hid_hbm.shape[0]
     dim = hid_hbm.shape[1]
     ff = w1.shape[1]
-    cap = back_hbm.shape[1]
+    piece = limit // PIECES
+    back_base = NQ * cap
     half_tok = tok // HALVES
     pair = 2 * cap
     nt = min(256, dim)
@@ -33,9 +35,13 @@
 
     def block_of(step):
         near = (0, 1, 2, 3)[step]
-        inner = (1, 2, 0, 3)[step]
+        inner = (1, 2, 3, 0)[step]
         pick = near + zz * (inner - near)
         return pick + mirror * (3 - 2 * pick)
+
+    def partner(c):
+        px, py = (q // 2) % 2, q // 4
+        return 2 * (py + (c // 2) * (1 - 2 * py)) + px + (c % 2) * (1 - 2 * px)
 
     def half(ref, h):
         return ref.at[pl.ds(h * half_tok, half_tok)]
@@ -69,12 +75,31 @@
             send_sem=p_send.at[peer], recv_sem=p_recv.at[step, peer],
             device_id=(z * NQ + peer,), device_id_type=MESH)
 
-    def back_copy(step, peer):
-        return pltpu.make_async_remote_copy(
-            src_ref=recv.at[step, pl.ds(peer * cap, cap)],
-            dst_ref=back_hbm.at[me],
-            send_sem=b_send.at[step, peer], recv_sem=b_recv.at[me],
-            device_id=(block_of(step) * NQ + peer,), device_id_type=MESH)
+    def landing(step, peer):
+        home = rows_hbm if step == 0 else land_hbm.at[step - 1]
+        return home.at[pl.ds(peer * cap, cap)]
+
+    def land_copy(step, peer):
+        return pltpu.make_async_remote_copy(
+            src_ref=recv.at[step, pl.ds(peer * cap, cap)], dst_ref=landing(step, q),
+            send_sem=l_send.at[step, peer], recv_sem=l_recv.at[step, q],
+            device_id=(z * NQ + peer,), device_id_type=MESH)
+
+    def land_arrival(step, peer):
+        return pltpu.make_async_remote_copy(
+            src_ref=recv.at[step, pl.ds(peer * cap, cap)], dst_ref=landing(step, peer),
+            send_sem=l_send.at[step, peer], recv_sem=l_recv.at[step, peer],
+            device_id=(z * NQ + peer,), device_id_type=MESH)
+
+    def land_own(step):
+        return pltpu.make_async_copy(recv.at[step, pl.ds(q * cap, cap)], landing(step, q), loc_sem.at[step])
+
+    def back_copy(step, g, plane, owner):
+        return pltpu.make_async_remote_copy(
+            src_ref=recv.at[step, pl.ds(g * piece, piece)],
+            dst_ref=rows_hbm.at[pl.ds(back_base + plane * limit + g * piece, piece)],
+            send_sem=b_send.at[step, g], recv_sem=b_recv.at[plane, g],
+            device_id=(owner * NQ + q,), device_id_type=MESH)
 
     own_load = pltpu.make_async_copy(hid_hbm, hid.at[z], own_sem)
     for h in range(HALVES):
@@ -108,10 +133,6 @@
         marked = jnp.where(chosen > 0.5, count, -1.0)
         for plane in range(NZ):
             rank[plane, :, span] = marked[plane * NQ:(plane + 1) * NQ]
-        slot0 = jnp.sum(jnp.where(first, count, 0.0), axis=0, keepdims=True).astype(jnp.int32)
-        slot1 = jnp.sum(jnp.where(second, count, 0.0), axis=0, keepdims=True).astype(jnp.int32)
-        pos_ref[pl.ds(0, 1), span] = ids_ref[pl.ds(0, 1), span] * cap + slot0
-        pos_ref[pl.ds(1, 1), span] = ids_ref[pl.ds(1, 1), span] * cap + slot1
     for plane in range(NZ):
         @pl.when(z != plane)
         def _():
@@ -120,6 +141,22 @@
         @pl.when(z == plane)
         def _():
             rank_in[plane] = rank[plane]
+
+    base = []
+    for plane in range(NZ):
+        run = jnp.zeros((1, 1), jnp.float32)
+        for e in range(NQ):
+            there = run + (back_base + plane * limit)
+            base.append(jnp.where(z == plane, float(e * cap), there))
+            run = run + carry[plane * NQ + e:plane * NQ + e + 1, :]
+    base = jnp.concatenate(base, axis=0)
+    for k in range(tok // lanes):
+        span = pl.ds(k * lanes, lanes)
+        place = jnp.concatenate([rank[plane, :, span] for plane in range(NZ)], axis=0) + base
+        for j in range(2):
+            hit = ids_ref[pl.ds(j, 1), span] == exp_iota
+            pos_ref[pl.ds(j, 1), span] = jnp.sum(
+                jnp.where(hit, place, 0.0), axis=0, keepdims=True).astype(jnp.int32)
 
     def relay(hop, h):
         @pl.when(z >= hop)
@@ -149,7 +186,7 @@
 
         @pl.loop(0, NQ // 2)
         def _(k):
-            p = (q // 2 + 1 + k) % (NQ // 2)
+            p = partner((k + 1) % (NQ // 2))
             for j in range(2):
                 peer = 2 * p + j
                 if step > 0:
@@ -177,11 +214,9 @@
                     recv[step, pl.ds(peer * cap, cap), :] = send[pl.ds(peer * cap, cap), :]
 
     def experts(step):
-        block = block_of(step)
-
         @pl.loop(0, NQ // 2)
         def _(k):
-            p = (q // 2 + NQ // 2 - k) % (NQ // 2)
+            p = partner(k)
             for j in range(2):
                 peer = 2 * p + j
 
@@ -206,15 +241,59 @@
 
             for j in range(2):
                 peer = 2 * p + j
-                home = block * NQ + peer
-
-                @pl.when(home != me)
+
+                @pl.when(peer != q)
                 def _():
-                    back_copy(step, peer).start()
-
-                @pl.when(home == me)
+                    land_copy(step, peer).start()
+
+                @pl.when(peer == q)
                 def _():
-                    pltpu.make_async_copy(recv.at[step, pl.ds(peer * cap, cap)], back_hbm.at[me], loc_sem).start()
+                    land_own(step).start()
+
+    def landed(step):
+        @pl.loop(0, NQ)
+        def _(peer):
+            @pl.when(peer != q)
+            def _():
+                land_arrival(step, peer).wait_recv()
+                land_copy(step, peer).wait_send()
+        land_own(step).wait()
+
+    def give_back(step):
+        block = block_of(step)
+        for h in range(HALVES):
+            @pl.when(jnp.logical_and(block < z, z < NZ - 1))
+            def _():
+                z_copy(0, z - block + 1, h, block).wait_send()
+
+            @pl.when(jnp.logical_and(block > z, z > 0))
+            def _():
+                z_copy(1, block - z + 1, h, block).wait_send()
+        landed(step)
+        stage = pltpu.make_async_copy(land_hbm.at[step - 1], hid.at[block], stage_sem)
+        stage.start()
+        slot_iota = lax.broadcasted_iota(jnp.int32, (1, cap), 1).astype(jnp.float32)
+        run = jnp.zeros((1, 1), jnp.float32)
+        for e in range(NQ):
+            taken = jnp.sum(jnp.where(rank_in[block, pl.ds(e, 1), :] >= 0.0, 1.0, 0.0), axis=1, keepdims=True)
+            slots[pl.ds(e, 1), :] = jnp.where(slot_iota < taken, slot_iota + run, -1.0)
+            run = run + taken
+        stage.wait()
+
+        @pl.loop(0, PIECES)
+        def _(g):
+            place = (lax.broadcasted_iota(jnp.int32, (piece, cap), 0) + g * piece).astype(jnp.float32)
+            for e in range(NQ):
+                sel[pl.ds(0, piece), pl.ds(e * cap, cap)] = jnp.where(
+                    place == slots[pl.ds(e, 1), :], 1.0, 0.0).astype(jnp.bfloat16)
+
+            @pl.loop(0, dim // nt)
+            def _(n):
+                cols = pl.ds(pl.multiple_of(n * nt, nt), nt)
+                recv[step, pl.ds(g * piece, piece), cols] = jnp.dot(
+                    sel[pl.ds(0, piece), :], hid[block, :, cols],
+                    preferred_element_type=jnp.float32).astype(jnp.bfloat16)
+            back_copy(step, g, z, block).start()
 
     own_load.wait()
     select(0)
@@ -225,16 +304,11 @@
         load.wait()
     experts(0)
     relay(2, 0)
-
-    @pl.when(zz == 0)
-    def _():
-        relay(2, 1)
+    experts(1)
+    relay(2, 1)
     select(2)
-    experts(1)
-
-    @pl.when(zz == 1)
-    def _():
-        relay(2, 1)
+    give_back(1)
+    experts(2)
     for h in range(HALVES):
         @pl.when(z >= 3)
         def _():
@@ -244,18 +318,18 @@
         def _():
             z_copy(1, 3, h, z + 3).wait_recv()
     select(3)
-    experts(2)
+    give_back(2)
     experts(3)
+    give_back(3)
 
     for h in range(HALVES):
-        for hop in range(1, NZ):
-            @pl.when(jnp.logical_and(z < NZ - 1, z >= hop - 1))
-            def _():
-                z_copy(0, hop, h, z - (hop - 1)).wait_send()
-
-            @pl.when(jnp.logical_and(z > 0, z + (hop - 1) < NZ))
-            def _():
-                z_copy(1, hop, h, z + (hop - 1)).wait_send()
+        @pl.when(z < NZ - 1)
+        def _():
+            z_copy(0, 1, h, z).wait_send()
+
+        @pl.when(z > 0)
+        def _():
+            z_copy(1, 1, h, z).wait_send()
     for plane in range(NZ):
         @pl.when(z != plane)
         def _():
@@ -266,22 +340,16 @@
         @pl.when(peer != q)
         def _():
             plane_copy(NZ - 1, peer).wait_send()
-        for step in range(NZ):
-            @pl.when(block_of(step) * NQ + peer != me)
-            def _():
-                back_copy(step, peer).wait_send()
-    pltpu.make_async_copy(recv.at[0, pl.ds(q * cap, cap)], back_hbm.at[me], loc_sem).wait()
-
-    @pl.loop(1, NZ * NQ)
-    def _(k):
-        other = (me + k) % (NZ * NQ)
-        pltpu.make_async_remote_copy(
-            src_ref=recv.at[0, pl.ds(0, cap)], dst_ref=back_hbm.at[other],
-            send_sem=b_send.at[0, 0], recv_sem=b_recv.at[other],
-            device_id=(other,), device_id_type=MESH).wait_recv()
-
-
-def moe_exchange(hidden_loc, ids_t, w_one, w_three, w_two, n):
+    landed(0)
+
+    @pl.loop(0, PIECES)
+    def _(g):
+        for step in range(1, NZ):
+            back_copy(step, g, z, block_of(step)).wait_send()
+            back_copy(step, g, block_of(step), block_of(step)).wait_recv()
+
+
+def moe_exchange(hidden_loc, ids_t, w_one, w_three, w_two, n, limit):
     tok, dim = hidden_loc.shape
     ff = w_one.shape[1]
     cap = 4 * tok // n
@@ -289,13 +357,14 @@
     vmem_spec = pl.BlockSpec(memory_space=pltpu.VMEM)
     dma = pltpu.SemaphoreType.DMA
     rows = n * cap
-    flops = 2 * rows * (3 * dim * ff + tok * dim)
+    flops = 2 * rows * (3 * dim * ff + 2 * tok * dim)
     return pl.pallas_call(
-        moe_kernel,
-        out_shape=(jax.ShapeDtypeStruct((n, cap, dim), jnp.bfloat16),
+        functools.partial(moe_kernel, limit, cap),
+        out_shape=(jax.ShapeDtypeStruct((NQ * cap + NZ * limit, dim), jnp.bfloat16),
+                   jax.ShapeDtypeStruct((NZ - 1, NQ * cap, dim), jnp.bfloat16),
                    jax.ShapeDtypeStruct((2, tok), jnp.int32)),
         in_specs=[any_spec, vmem_spec, any_spec, any_spec, any_spec],
-        out_specs=(any_spec, vmem_spec),
+        out_specs=(any_spec, any_spec, vmem_spec),
         scratch_shapes=[
             pltpu.VMEM((NZ, tok, dim), jnp.bfloat16),
             pltpu.VMEM((NQ * cap, dim), jnp.bfloat16),
@@ -307,13 +376,52 @@
             pltpu.VMEM((2 * cap, tok), jnp.bfloat16),
             pltpu.VMEM((NZ, NQ, tok), jnp.float32),
             pltpu.VMEM((NZ, NQ, tok), jnp.float32),
+            pltpu.VMEM((NQ, cap), jnp.float32),
             dma(()), dma((3,)), dma((2, NZ - 1, HALVES)), dma((2, NZ - 1, HALVES)),
             dma((NZ,)), dma((NZ,)), dma((NQ,)), dma((NZ, NQ)),
-            dma((NZ, NQ)), dma((NZ * NQ,)), dma(()),
+            dma((NZ, NQ)), dma((NZ, NQ)), dma((NZ,)), dma(()),
+            dma((NZ, PIECES)), dma((NZ, PIECES)),
         ],
         compiler_params=pltpu.CompilerParams(has_side_effects=True, vmem_limit_bytes=67043328),
         cost_estimate=pl.CostEstimate(flops=flops, bytes_accessed=2 * rows * dim * 4, transcendentals=rows * ff),
     )(hidden_loc, ids_t, w_one, w_three, w_two)
+
+
+def most_kernel(n, mine_ref, most_ref, theirs, send_sem, recv_sem):
+    me = lax.axis_index("ep")
+
+    def copy(slot, target):
+        return pltpu.make_async_remote_copy(
+            src_ref=mine_ref, dst_ref=theirs.at[slot],
+            send_sem=send_sem.at[target], recv_sem=recv_sem.at[slot],
+            device_id=(target,), device_id_type=MESH)
+
+    theirs[me] = mine_ref[...]
+
+    @pl.loop(1, n)
+    def _(k):
+        copy(me, (me + k) % n).start()
+
+    @pl.loop(1, n)
+    def _(k):
+        copy((me + k) % n, (me + k) % n).wait_recv()
+
+    @pl.loop(1, n)
+    def _(k):
+        copy(me, (me + k) % n).wait_send()
+    most_ref[...] = jnp.max(theirs[...], axis=0)
+
+
+def most_of_all(mine, n):
+    vmem_spec = pl.BlockSpec(memory_space=pltpu.VMEM)
+    return pl.pallas_call(
+        functools.partial(most_kernel, n),
+        out_shape=jax.ShapeDtypeStruct(mine.shape, mine.dtype),
+        in_specs=[vmem_spec], out_specs=vmem_spec,
+        scratch_shapes=[pltpu.VMEM((n, *mine.shape), mine.dtype),
+                        pltpu.SemaphoreType.DMA((n,)), pltpu.SemaphoreType.DMA((n,))],
+        compiler_params=pltpu.CompilerParams(has_side_effects=True),
+    )(mine)
 
 
 def route_gates(hidden_loc, w_router, ids_loc):
@@ -330,12 +438,21 @@
     n = mesh.shape["ep"]
 
     def device_body(hidden_loc, w_router, ids_loc, w_one, w_three, w_two):
-        dim = hidden_loc.shape[1]
-        back, pos = moe_exchange(hidden_loc, ids_loc.T, w_one[0], w_three[0], w_two[0], n)
-        flat = back.reshape(-1, dim)
+        tok, dim = hidden_loc.shape
         g_a, g_b = route_gates(hidden_loc, w_router, ids_loc)
-        e_a = jnp.take(flat, pos[0], axis=0, mode="clip").astype(jnp.float32)
-        e_b = jnp.take(flat, pos[1], axis=0, mode="clip").astype(jnp.float32)
-        return (g_a * e_a + g_b * e_b).astype(jnp.bfloat16)
+        ids_t = ids_loc.T
+
+        def run(limit):
+            rows, _, pos = moe_exchange(hidden_loc, ids_t, w_one[0], w_three[0], w_two[0], n, limit)
+            both = lax.optimization_barrier(jnp.take(rows, pos.reshape(-1), axis=0, mode="clip"))
+            e_a, e_b = both[:tok].astype(jnp.float32), both[tok:].astype(jnp.float32)
+            return (g_a * e_a + g_b * e_b).astype(jnp.bfloat16)
+
+        in_plane = ids_t[None] // NQ == jnp.arange(NZ)[:, None, None]
+        choices = jnp.max(jnp.sum(in_plane.astype(jnp.float32), axis=(1, 2)))
+        most = most_of_all(jnp.full((8, 128), choices, jnp.float32), n)
+        limits = (tok * 5 // 8, tok * 11 // 16, tok)
+        level = sum((most[0, 0] > limit).astype(jnp.int32) for limit in limits[:-1])
+        return lax.switch(level, [functools.partial(run, limit) for limit in limits])
 
     return jax.shard_map(device_body, mesh=mesh, in_specs=(P("ep", None), P(None, None), P("ep", None), P("ep", None, None), P("ep", None, None), P("ep", None, None)), out_specs=P("ep", None), check_vma=False)

time: 733 us -> 654 us (0.89)
  Pallas kernels: 686 us -> 603 us
    pallas_call x1 -> x2, Pallas kernels: 686 us -> 603 us  [the longest x1 590 us: moe_exchange(): pl.pallas_call(functools.partial(moe_kernel, limit, cap), out_shape=(jax....]
    gather x2 -> x1, local copies, waits for them, and re-layouts: 38 us -> 28.3 us  [run(): jnp.take(rows, pos.reshape(-1), axis=0, mode='clip')]
where the time goes in v2:
time: 654 us; the launch traced here: 656 us
  Pallas kernels  603 us (92%)
  local copies, waits for them, and re-layouts  34.9 us (5%)
  other arithmetic  6.7 us (1%)
    pallas_call x1, Pallas kernels, moe_exchange(): pl.pallas_call(functools.partial(moe_kernel, limit, cap), out_shape=(jax....  590 us
    gather x1, local copies, waits for them, and re-layouts, run(): jnp.take(rows, pos.reshape(-1), axis=0, mode='clip')  28.3 us
    pallas_call x1, Pallas kernels, most_of_all(): pl.pallas_call(functools.partial(most_kernel, n), out_shape=jax.ShapeDtyp...  13.1 us

profile of v2, /device:TPU:27, one launch (start us, length us, event | category | flops | bytes accessed | tf_op | source)
XLA Modules:
  0.0 656.2 jit_solution(9057818238767971710)
XLA Ops:
  0.0 3.5 fusion.6
  3.5 0.1 fusion.1
  3.6 0.8 fusion.5
  4.4 0.1 select_reduce_fusion
  4.6 0.0 copy-start.1
  4.6 0.0 copy-start.5
  4.6 0.6 copy-done.1
  5.1 0.6 add.31
  5.7 0.0 copy-done.5
  5.7 0.8 and_select_fusion
  6.5 0.1 convert_reduce_fusion
  6.7 0.7 reduce_max.18
  7.3 1.3 broadcast_in_dim.26.mine_ref
  8.6 13.1 %shard_map.88 = f32[8,128]{1,0:T(8,128)} custom-call(f32[8,128]{1,0:T(8,128)} %broadcast_in_dim.26.mine_ref), custom_call_target="tpu_custom_call" | custom-call | tf_op jit(solution)/shard_map/pallas_call | solution.py:417
  21.7 1.2 slice.28
  24.1 629.5 %conditional.8 = (bf16[2048,1024]{1,0:T(8,128)(2,1)S(1)}) conditional(s32[]{:T(128)} %bitcast.1, (f32[2048,1]{0,1:T(1,128)}, bf16[1,1024,2816]{2,1,0:T(8,128)(2,1)}, bf16[1,1024,2816]{2,1,0:T(8,128)(2,1)}, bf16[1,2816,1024]{2,1,0:T(8,128)(2,1)}, bf16[2048,1024]{1,0:T(8,128)(2,1)}, /*index=5*/s32[2,2048]{1,0:T(2,128)}, ...), branch_computations={%region_6.7_spmd.clone, %region_7.8_spmd.clone, %region_8.9_spmd.c... | conditional | flops 210465980416 | bytes 96706656
  24.2 590.2 %branch_1_fun.1 = (bf16[7680,1024]{1,0:T(8,128)(2,1)}, bf16[3,2048,1024]{2,1,0:T(8,128)(2,1)}, s32[2,2048]{1,0:T(2,128)}) custom-call(bf16[2048,1024]{1,0:T(8,128)(2,1)} %get-tuple-element.134.hid_hbm, s32[2,2048]{1,0:T(2,128)} %get-tuple-element.135.ids_ref, bf16[1024,2816]{1,0:T(8,128)(2,1)} %bitcast.56, bf16[1024,2816]{1,0:T(8,128)(2,1)} %bitcast.59, ...), custom_call_target="tpu_custom_call" | custom-call | flops 210453397504 | bytes 67108864 | tf_op jit(solution)/shard_map/cond/branch_1_fun/pallas_call | solution.py:361
  614.4 0.7 copy.32
  615.2 0.0 copy-start.3
  615.2 0.0 copy-start.7
  615.2 0.0 copy-start.10
  615.2 28.3 %gather_fusion.1 = bf16[4096,1024]{1,0:T(8,128)(2,1)} fusion(bf16[7680,1024]{1,0:T(8,128)(2,1)} %get-tuple-element.136, s32[4096]{0:T(1024)S(1)} %broadcast_clamp_fusion.1), kind=kCustom, calls=%fused_computation.1 | custom fusion | bytes 16793600 | tf_op jit(solution)/shard_map/cond/branch_1_fun/jit(_take)/gather | solution.py:447
  643.5 0.0 copy-done.3
  643.5 0.0 copy-done.7
  643.5 0.0 copy-done.10
  643.5 4.3 multiply_add_fusion.1
  653.6 0.0 copy-start
  653.6 2.0 copy-done
  (2 shorter events, 0.0 us)
Async XLA Ops:
  4.6 0.6 copy-start.1
  4.6 1.2 copy-start.5
  615.2 28.3 %copy-start.3 = (f32[2048,1]{0,1:T(1,128)S(1)}, f32[2048,1]{0,1:T(1,128)}, u32[]{:S(2)}) copy-start(f32[2048,1]{0,1:T(1,128)} %get-tuple-element.140) | copy-start | bytes 24580
  615.2 28.3 %copy-start.7 = (f32[2048,1]{0,1:T(1,128)S(1)}, f32[2048,1]{0,1:T(1,128)}, u32[]{:S(2)}) copy-start(f32[2048,1]{0,1:T(1,128)} %get-tuple-element.138) | copy-start | bytes 24580
  615.2 28.3 %copy-start.10 = (f32[2048,1]{0,1:T(1,128)S(1)}, f32[2048,1]{0,1:T(1,128)}, u32[]{:S(2)}) copy-start(f32[2048,1]{0,1:T(1,128)} %get-tuple-element.139) | copy-start | bytes 24580
  653.6 2.0 copy-start

commit v3 on v2

--- a/solution.py
+++ b/solution.py
@@ -35,7 +35,7 @@
 
     def block_of(step):
         near = (0, 1, 2, 3)[step]
-        inner = (1, 2, 3, 0)[step]
+        inner = (1, 2, 0, 3)[step]
         pick = near + zz * (inner - near)
         return pick + mirror * (3 - 2 * pick)
 
@@ -451,7 +451,7 @@
         in_plane = ids_t[None] // NQ == jnp.arange(NZ)[:, None, None]
         choices = jnp.max(jnp.sum(in_plane.astype(jnp.float32), axis=(1, 2)))
         most = most_of_all(jnp.full((8, 128), choices, jnp.float32), n)
-        limits = (tok * 5 // 8, tok * 11 // 16, tok)
+        limits = (tok * 19 // 32, tok * 11 // 16, tok)
         level = sum((most[0, 0] > limit).astype(jnp.int32) for limit in limits[:-1])
         return lax.switch(level, [functools.partial(run, limit) for limit in limits])
 

time: 654 us -> 604 us (0.924)
  Pallas kernels: 603 us -> 556 us
    pallas_call x1, Pallas kernels: 590 us -> 543 us  [moe_exchange(): pl.pallas_call(functools.partial(moe_kernel, limit, cap), out_shape=(jax....]
where the time goes in v3:
time: 604 us; the launch traced here: 602 us
  Pallas kernels  556 us (92%)
  local copies, waits for them, and re-layouts  34.2 us (6%)
  other arithmetic  6.7 us (1%)
    pallas_call x1, Pallas kernels, moe_exchange(): pl.pallas_call(functools.partial(moe_kernel, limit, cap), out_shape=(jax....  543 us
    gather x1, local copies, waits for them, and re-layouts, run(): jnp.take(rows, pos.reshape(-1), axis=0, mode='clip')  27.6 us
    pallas_call x1, Pallas kernels, most_of_all(): pl.pallas_call(functools.partial(most_kernel, n), out_shape=jax.ShapeDtyp...  13.1 us

profile of v3, /device:TPU:27, one launch (start us, length us, event | category | flops | bytes accessed | tf_op | source)
XLA Modules:
  0.0 602.1 jit_solution(5130232660821626507)
XLA Ops:
  0.0 3.5 fusion.6
  3.5 0.1 fusion.1
  3.6 0.8 fusion.5
  4.4 0.1 select_reduce_fusion
  4.6 0.0 copy-start.1
  4.6 0.0 copy-start.5
  4.6 0.6 copy-done.1
  5.1 0.6 add.31
  5.7 0.0 copy-done.5
  5.7 0.8 and_select_fusion
  6.5 0.1 convert_reduce_fusion
  6.7 0.7 reduce_max.18
  7.3 1.3 broadcast_in_dim.26.mine_ref
  8.6 13.1 %shard_map.88 = f32[8,128]{1,0:T(8,128)} custom-call(f32[8,128]{1,0:T(8,128)} %broadcast_in_dim.26.mine_ref), custom_call_target="tpu_custom_call" | custom-call | tf_op jit(solution)/shard_map/pallas_call | solution.py:417
  21.7 1.2 slice.28
  24.1 576.0 %conditional.8 = (bf16[2048,1024]{1,0:T(8,128)(2,1)S(1)}) conditional(s32[]{:T(128)} %bitcast.1, (f32[2048,1]{0,1:T(1,128)}, bf16[1,1024,2816]{2,1,0:T(8,128)(2,1)}, bf16[1,1024,2816]{2,1,0:T(8,128)(2,1)}, bf16[1,2816,1024]{2,1,0:T(8,128)(2,1)}, bf16[2048,1024]{1,0:T(8,128)(2,1)}, /*index=5*/s32[2,2048]{1,0:T(2,128)}, ...), branch_computations={%region_6.7_spmd.clone, %region_7.8_spmd.clone, %region_8.9_spmd.c... | conditional | flops 210465980416 | bytes 96706656
  24.1 542.8 %branch_0_fun.1 = (bf16[6912,1024]{1,0:T(8,128)(2,1)}, bf16[3,2048,1024]{2,1,0:T(8,128)(2,1)}, s32[2,2048]{1,0:T(2,128)}) custom-call(bf16[2048,1024]{1,0:T(8,128)(2,1)} %get-tuple-element.115.hid_hbm, s32[2,2048]{1,0:T(2,128)} %get-tuple-element.116.ids_ref, bf16[1024,2816]{1,0:T(8,128)(2,1)} %bitcast.55, bf16[1024,2816]{1,0:T(8,128)(2,1)} %bitcast.58, ...), custom_call_target="tpu_custom_call" | custom-call | flops 210453397504 | bytes 67108864 | tf_op jit(solution)/shard_map/cond/branch_0_fun/pallas_call | solution.py:361
  566.8 0.7 copy.31
  567.5 0.0 copy-start.2
  567.6 0.0 copy-start.6
  567.6 0.0 copy-start.9
  567.6 27.6 %gather_fusion = bf16[4096,1024]{1,0:T(8,128)(2,1)} fusion(bf16[6912,1024]{1,0:T(8,128)(2,1)} %get-tuple-element.117, s32[4096]{0:T(1024)S(1)} %broadcast_clamp_fusion), kind=kCustom, calls=%fused_computation | custom fusion | bytes 16793600 | tf_op jit(solution)/shard_map/cond/branch_0_fun/jit(_take)/gather | solution.py:447
  595.2 0.0 copy-done.2
  595.2 0.0 copy-done.6
  595.2 0.0 copy-done.9
  595.2 4.3 multiply_add_fusion
  600.1 0.0 copy-start
  600.1 2.0 copy-done
  (2 shorter events, 0.0 us)
Async XLA Ops:
  4.6 0.6 copy-start.1
  4.6 1.2 copy-start.5
  567.5 27.6 %copy-start.2 = (f32[2048,1]{0,1:T(1,128)S(1)}, f32[2048,1]{0,1:T(1,128)}, u32[]{:S(2)}) copy-start(f32[2048,1]{0,1:T(1,128)} %get-tuple-element.121) | copy-start | bytes 24580
  567.6 27.6 %copy-start.6 = (f32[2048,1]{0,1:T(1,128)S(1)}, f32[2048,1]{0,1:T(1,128)}, u32[]{:S(2)}) copy-start(f32[2048,1]{0,1:T(1,128)} %get-tuple-element.119) | copy-start | bytes 24580
  567.6 27.6 %copy-start.9 = (f32[2048,1]{0,1:T(1,128)S(1)}, f32[2048,1]{0,1:T(1,128)}, u32[]{:S(2)}) copy-start(f32[2048,1]{0,1:T(1,128)} %get-tuple-element.120) | copy-start | bytes 24580
  600.1 2.0 copy-start
